TPU v7x, 512 devices: a whole 4x8x8 slice. The times are simulated.
512 devices in a mesh: row: 16 (over y, core), col: 32 (over z, x).
Axes of the slice: x: 4, y: 8, z: 8, core: 2. Of those that a mesh axis runs over, the one named last changes fastest.
Arguments:
- templates: float32 [1536, 3, 1024], P(('row', 'col')), may hold values from -600 to 600
Outputs:
- similar: float32 [1536, 1536], P(('row', 'col'))
All inputs are finite; a program needn't handle non-finite values.
Results may differ from a plain program's by a relative error of at most 0.0012.
Values may be sent and summed in bfloat16 or wider, within the bound.
No kernel may reach another device: no remote copies, remote signals or barrier semaphores. Data moves between devices by JAX's collectives and lax.ppermute only.
A program may use at most 128 MiB of HBM per device.

v0:
```python
import math
import jax
import jax.numpy as jnp
from jax import lax
from jax.sharding import PartitionSpec as P

LAGS = 512


def copy_for_each(array, axis):
    copies = jnp.broadcast_to(array, (lax.axis_size(axis), *array.shape))
    return lax.all_to_all(copies, axis, split_axis=0, concat_axis=0, tiled=True)


def in_order(tiles, dim):
    shape = list(tiles.shape[1:])
    shape[dim] *= tiles.shape[0]
    return jnp.moveaxis(tiles, 0, dim).reshape(shape)


def collect(array, axis, dim):
    tiles = copy_for_each(array, axis)
    return in_order(tiles, dim)


def normalize(templates):
    scaling = lax.rsqrt(jnp.mean(templates * templates, axis=2, keepdims=True) + 1e-06) / math.sqrt(
        templates.shape[2]
    )
    return (templates * scaling).astype(jnp.bfloat16)


def forward_table(samples, transform_len):
    half_len = transform_len // 2
    sample_idx = jnp.arange(samples, dtype=jnp.int32)[:, None]
    slot_idx = jnp.arange(transform_len, dtype=jnp.int32)[None, :]
    freq_idx = jnp.where(slot_idx < half_len, slot_idx, slot_idx - half_len)
    phases = sample_idx * freq_idx % transform_len
    angles = phases.astype(jnp.float32) * (2.0 * math.pi / transform_len)
    nyquist = jnp.where(sample_idx % 2 == 0, 1.0, -1.0)
    basis = jnp.where(
        slot_idx < half_len,
        jnp.cos(angles),
        jnp.where(slot_idx == half_len, nyquist, -jnp.sin(angles)),
    )
    return basis.astype(jnp.bfloat16)


def inverse_table(transform_len, lag_total):
    half_len = transform_len // 2
    slot_idx = jnp.arange(transform_len, dtype=jnp.int32)[:, None]
    lag_idx = jnp.arange(lag_total, dtype=jnp.int32)[None, :] - lag_total // 2
    freq_idx = jnp.where(slot_idx < half_len, slot_idx, slot_idx - half_len)
    phases = freq_idx * lag_idx % transform_len
    angles = phases.astype(jnp.float32) * (2.0 * math.pi / transform_len)
    weight = jnp.where(freq_idx == 0, 1.0, 2.0) / transform_len
    nyquist = jnp.where(lag_idx % 2 == 0, 1.0, -1.0) / transform_len
    basis = jnp.where(
        slot_idx < half_len,
        weight * jnp.cos(angles),
        jnp.where(slot_idx == half_len, nyquist, -weight * jnp.sin(angles)),
    )
    return basis.astype(jnp.bfloat16)


def spectra_of(normed, basis):
    row_total, comps, samples = normed.shape
    flattened = normed.reshape(row_total * comps, samples)
    spectrum = jnp.dot(flattened, basis, preferred_element_type=jnp.float32)
    return spectrum.astype(jnp.bfloat16).reshape(row_total, comps, basis.shape[1])


def pair_einsum(left_part, right_part):
    return jnp.einsum("icf,jcf->ijf", left_part.astype(jnp.float32), right_part.astype(jnp.float32))


def similarity(left_spec, right_spec, inverse):
    half_len = left_spec.shape[2] // 2
    left_real = left_spec[:, :, :half_len]
    left_imag = left_spec[:, :, half_len:]
    right_real = right_spec[:, :, :half_len]
    right_imag = right_spec[:, :, half_len:]
    above_zero = jnp.arange(half_len, dtype=jnp.int32) >= 1
    right_masked = jnp.where(above_zero, right_imag, jnp.zeros_like(right_imag))
    left_masked = jnp.where(above_zero, left_real, jnp.zeros_like(left_real))
    right_turned = jnp.where(above_zero, -right_real, right_imag)
    even_part = pair_einsum(
        jnp.concatenate([left_real, left_imag], axis=1),
        jnp.concatenate([right_real, right_masked], axis=1),
    )
    odd_part = pair_einsum(
        jnp.concatenate([left_masked, left_imag], axis=1),
        jnp.concatenate([right_imag, right_turned], axis=1),
    )
    cross_spec = jnp.concatenate([even_part, odd_part], axis=2).astype(jnp.bfloat16)
    left_rows = left_spec.shape[0]
    right_rows = right_spec.shape[0]
    lagged = jnp.dot(
        cross_spec.reshape(left_rows * right_rows, 2 * half_len),
        inverse,
        preferred_element_type=jnp.float32,
    )
    return jnp.max(lagged, axis=1).reshape(left_rows, right_rows)


def body(templates):
    per_device = templates.shape[0]
    samples = templates.shape[2]
    transform_len = samples + LAGS // 2
    forward = forward_table(samples, transform_len)
    inverse = inverse_table(transform_len, LAGS)
    local_waves = normalize(templates)
    outgoing = spectra_of(local_waves, forward)
    row_count = lax.axis_size("row")
    col_count = lax.axis_size("col")
    partners = collect(outgoing, "row", 0)
    pair_block = similarity(collect(outgoing, "col", 0), partners, inverse)
    owned_rows = lax.all_to_all(pair_block, "col", split_axis=0, concat_axis=1, tiled=True)
    reordered = owned_rows.reshape(per_device, col_count, row_count, per_device).transpose(
        0, 2, 1, 3
    )
    return reordered.reshape(per_device, col_count * row_count * per_device)


def solution(mesh):
    placed = (P(("row", "col"), None, None),)
    return jax.shard_map(
        body, mesh=mesh, in_specs=placed, out_specs=P(("row", "col"), None), check_vma=False
    )
```

profile of v0, /device:TPU:1, one launch (start us, length us, event | category | flops | bytes accessed | tf_op | source)
XLA Modules:
  0.0 158.0 jit_solution(2501880423134903222)
XLA Ops:
  0.0 0.9 multiply_reduce_fusion
  0.9 0.9 multiply_convert_fusion
  1.8 22.6 %fusion.20 = bf16[9,1280]{1,0:T(8,128)(2,1)S(1)} fusion(bf16[9,1024]{1,0:T(8,128)(2,1)S(1)} %reshape.135, bf16[1024]{0:T(1024)(128)(2,1)S(1)} %fusion.37, s32[1280]{0:T(1024)S(1)} %add_select_fusion.2, pred[1280]{0:T(1024)(128)(4,1)S(1)} %get-tuple-element.11, pred[1280]{0:T(1024)(128)(4,1)S(1)} %get-tuple-element.12), kind=kOutput, calls=%fused_computation.26 | convolution fusion | flops 39333120 | bytes 51200 | tf_op jit(solution)/shard_map/dot_general | solution.py:69
  24.5 0.1 broadcast_in_dim.105
  24.6 25.9 %all_to_all.26 = bf16[16,3,3,1280]{3,1,2,0:T(4,128)(2,1)S(1)} all-to-all(bf16[16,3,3,1280]{3,1,2,0:T(4,128)(2,1)S(1)} %broadcast_in_dim.105), channel_id=1, replica_groups=mesh['row'=16,'col'=32] {'row'}, dimensions={0} | all-to-all | bytes 737280 | tf_op jit(solution)/shard_map/all_to_all | solution.py:12
  50.5 1.2 broadcast_in_dim.108
  51.7 12.1 %all-to-all-start.1 = ((bf16[32,3,3,1280]{3,1,2,0:T(4,128)(2,1)}), bf16[32,3,3,1280]{3,1,2,0:T(4,128)(2,1)S(1)}, u32[]{:S(2)}, u32[]{:S(2)}) async-start(bf16[32,3,3,1280]{3,1,2,0:T(4,128)(2,1)} %broadcast_in_dim.108), calls=%async_computation.1 | async-start | bytes 1966080 | tf_op jit(solution)/shard_map/all_to_all | solution.py:12
  63.9 13.3 %select_convert_fusion.11 = bf16[1280,512]{1,0:T(8,128)(2,1)} fusion(f32[1280]{0:T(1024)S(1)} %get-tuple-element.14, bf16[512]{0:T(512)(128)(2,1)S(1)} %select_multiply_fusion.1, s32[512]{0:T(512)S(1)} %iota_add_fusion, s32[1280]{0:T(1024)S(1)} %add_select_fusion.2, f32[1280]{0:T(1024)S(1)} %get-tuple-element.13, ...), kind=kLoop, calls=%fused_computation.17.clone.clone.2 | loop fusion | flops 8519680 | bytes 1331712 | tf_op jit(solution)/shard_map/dot_general | solution.py:98
  77.2 0.2 copy.15
  77.4 0.3 reshape.137
  77.7 0.1 broadcast_select_fusion.1
  77.8 1.3 copy.22
  79.2 1.8 %copy.20 = bf16[48,6,640]{0,1,2:T(8,128)(2,1)} copy(bf16[48,6,640]{2,0,1:T(8,128)(2,1)S(1)} %pad_maximum_fusion.4) | data formatting | bytes 737280 | tf_op jit(solution)/shard_map/concatenate | solution.py:89
  81.0 9.1 %all-to-all-done.1 = bf16[32,3,3,1280]{3,1,2,0:T(4,128)(2,1)S(1)} async-done(((bf16[32,3,3,1280]{3,1,2,0:T(4,128)(2,1)}), bf16[32,3,3,1280]{3,1,2,0:T(4,128)(2,1)S(1)}, u32[]{:S(2)}, u32[]{:S(2)}) %all-to-all-start.1) | async-done | bytes 737312 | tf_op jit(solution)/shard_map/all_to_all | solution.py:12
  90.1 1.3 copy.17
  91.4 2.3 %reshape.138 = bf16[96,3,1280]{2,0,1:T(8,128)(2,1)S(1)} reshape(bf16[32,3,3,1280]{3,1,0,2:T(4,128)(2,1)} %copy.17) | data formatting | bytes 1474560 | tf_op jit(solution)/shard_map/reshape | solution.py:18
  93.7 0.8 fusion.50
  94.6 0.8 copy.26
  95.4 2.4 %broadcast_select_fusion = bf16[96,3,640]{0,1,2:T(4,128)(2,1)S(1)} fusion(bf16[96,3,640]{0,1,2:T(4,128)(2,1)S(1)} %copy.26, pred[640]{0:T(1024)(128)(4,1)S(1)} %iota_compare_fusion.2), kind=kLoop, calls=%fused_computation.41 | loop fusion | flops 184320 | bytes 737920 | tf_op jit(solution)/shard_map/jit(_where)/select_n | solution.py:85
  97.8 1.7 %copy.27 = bf16[96,3,640]{0,1,2:T(4,128)(2,1)S(1)} copy(bf16[96,3,640]{2,0,1:T(8,128)(2,1)} %get-tuple-element.6) | data formatting | bytes 737280
  99.4 4.5 %convert_bitcast_fusion = bf16[96,48,640]{0,1,2:T(8,128)(2,1)} fusion(bf16[48,6,640]{0,1,2:T(8,128)(2,1)S(1)} %copy.22, bf16[96,3,640]{0,1,2:T(4,128)(2,1)S(1)} %copy.27, bf16[96,3,640]{0,1,2:T(4,128)(2,1)S(1)} %broadcast_select_fusion), kind=kOutput, calls=%fused_computation.4 | convolution fusion | flops 39813120 | bytes 7004160 | tf_op jit(solution)/shard_map/icf,jcf->ijf/dot_general | solution.py:74
  103.9 0.0 copy-start
  103.9 11.5 %copy.23 = bf16[96,48,640]{2,1,0:T(8,128)(2,1)} copy(bf16[96,48,640]{0,1,2:T(8,128)(2,1)} %convert_bitcast_fusion) | data formatting | bytes 11796480 | tf_op jit(solution)/shard_map/icf,jcf->ijf/transpose | solution.py:74
  115.4 0.0 copy-done
  115.4 4.5 %convert_bitcast_fusion.1 = bf16[96,48,640]{0,1,2:T(8,128)(2,1)} fusion(bf16[48,6,640]{0,1,2:T(8,128)(2,1)S(1)} %copy-done, bf16[96,3,640]{0,1,2:T(4,128)(2,1)S(1)} %copy.27, bf16[96,3,640]{0,1,2:T(4,128)(2,1)S(1)} %copy.26), kind=kOutput, calls=%fused_computation.5 | convolution fusion | flops 39813120 | bytes 7004160 | tf_op jit(solution)/shard_map/icf,jcf->ijf/dot_general | solution.py:74
  119.8 0.0 copy-start.1
  119.8 11.4 %copy.21 = bf16[96,48,640]{2,1,0:T(8,128)(2,1)} copy(bf16[96,48,640]{0,1,2:T(8,128)(2,1)} %convert_bitcast_fusion.1) | data formatting | bytes 11796480 | tf_op jit(solution)/shard_map/icf,jcf->ijf/transpose | solution.py:74
  131.2 0.0 copy-done.1
  131.2 9.6 %fusion.17 = f32[4608]{0:T(1024)S(1)} fusion(bf16[4608,640]{1,0:T(8,128)(2,1)} %bitcast.21, bf16[4608,640]{1,0:T(8,128)(2,1)} %bitcast.22, bf16[1280,512]{1,0:T(8,128)(2,1)S(1)} %copy-done.1), kind=kOutput, calls=%fused_computation.25 | convolution fusion | flops 6065745408 | bytes 13125632 | tf_op jit(solution)/shard_map/dot_general | solution.py:98
  140.9 0.1 all_to_all.20
  141.0 0.1 reshape.141
  141.1 14.0 %all_to_all.27 = f32[32,1,144]{2,1,0:T(1,128)S(1)} all-to-all(f32[32,1,144]{2,1,0:T(1,128)S(1)} %reshape.141), channel_id=1, replica_groups=mesh['row'=16,'col'=32] {'col'}, dimensions={0} | all-to-all | bytes 36864 | tf_op jit(solution)/shard_map/all_to_all | solution.py:118
  155.1 0.5 broadcast.247
  155.6 0.7 reduce
  156.3 0.1 reshape.142
  156.4 0.1 copy.24
  156.6 0.4 copy.25
  156.9 1.1 reshape.140
  (14 shorter events, 0.2 us)
Async XLA Ops:
  51.7 38.4 %all-to-all-start.1 = ((bf16[32,3,3,1280]{3,1,2,0:T(4,128)(2,1)}), bf16[32,3,3,1280]{3,1,2,0:T(4,128)(2,1)S(1)}, u32[]{:S(2)}, u32[]{:S(2)}) async-start(bf16[32,3,3,1280]{3,1,2,0:T(4,128)(2,1)} %broadcast_in_dim.108), calls=%async_computation.1 | async-start | bytes 1966080 | tf_op jit(solution)/shard_map/all_to_all | solution.py:12
  103.9 11.5 %copy-start = (bf16[48,6,640]{0,1,2:T(8,128)(2,1)S(1)}, bf16[48,6,640]{0,1,2:T(8,128)(2,1)}, u32[]{:S(2)}) copy-start(bf16[48,6,640]{0,1,2:T(8,128)(2,1)} %copy.20) | copy-start | bytes 1105924
  119.8 11.4 %copy-start.1 = (bf16[1280,512]{1,0:T(8,128)(2,1)S(1)}, bf16[1280,512]{1,0:T(8,128)(2,1)}, u32[]{:S(2)}) copy-start(bf16[1280,512]{1,0:T(8,128)(2,1)} %select_convert_fusion.11) | copy-start | bytes 3932164
where the time goes:
time: 159 us; the launch traced here: 158 us
  matrix products  41.2 us (26%)
  blocking collectives  39.9 us (25%)
  local copies, waits for them, and re-layouts  37.2 us (23%)
  other arithmetic  18.4 us (12%)
  starting transfers between devices  12.1 us (8%)
  waiting for transfers between devices  9.09 us (6%)
    all_to_all x1, blocking collectives, copy_for_each(): return lax.all_to_all(copies, axis, split_axis=0, concat_axis=0, tiled=True)  25.9 us
    transpose x2, local copies, waits for them, and re-layouts, pair_einsum(): jnp.einsum('icf,jcf->ijf', left_part.astype(jnp.float32), right_part.asty...  22.9 us
    dot_general x1, matrix products, spectra_of(): spectrum = jnp.dot(flattened, basis, preferred_element_type=jnp.float32)  22.6 us
    all_to_all x1, blocking collectives, body(): lax.all_to_all(pair_block, 'col', split_axis=0, concat_axis=1, tiled=True)  14 us
    dot_general x1, other arithmetic, similarity(): jnp.dot(cross_spec.reshape(left_rows * right_rows, 2 * half_len), inverse...  13.3 us
    all_to_all x1, starting transfers between devices, copy_for_each(): return lax.all_to_all(copies, axis, split_axis=0, concat_axis=0, tiled=True)  12.1 us
    dot_general x1, matrix products, similarity(): jnp.dot(cross_spec.reshape(left_rows * right_rows, 2 * half_len), inverse...  9.65 us
    all_to_all x1, waiting for transfers between devices, copy_for_each(): return lax.all_to_all(copies, axis, split_axis=0, concat_axis=0, tiled=True)  9.09 us
  transfers between devices with their start and end apart: 1, of which 1 were waited for; matrix products, arithmetic and copies ran while one was open for 11% of the time, Pallas kernels for 0%

commit v1 on v0

--- a/solution.py
+++ b/solution.py
@@ -115,7 +115,10 @@
     col_count = lax.axis_size("col")
     partners = collect(outgoing, "row", 0)
     pair_block = similarity(collect(outgoing, "col", 0), partners, inverse)
-    owned_rows = lax.all_to_all(pair_block, "col", split_axis=0, concat_axis=1, tiled=True)
+    size = lax.axis_size("col")
+    parts = jnp.stack(jnp.split(pair_block, size, axis=0), axis=0)
+    parts = lax.all_to_all(parts, "col", split_axis=0, concat_axis=0)
+    owned_rows = jnp.concatenate(parts, axis=1)
     reordered = owned_rows.reshape(per_device, col_count, row_count, per_device).transpose(
         0, 2, 1, 3
     )

time: 159 us -> 162 us (1.019)
  local copies, waits for them, and re-layouts: 37.2 us -> 40.3 us
    another operation x0 -> x34, local copies, waits for them, and re-layouts: none -> 2.67 us  [the longest x33 2.64 us: body(): parts = jnp.stack(jnp.split(pair_block, size, axis=0), axis=0)]
where the time goes in v1:
time: 162 us; the launch traced here: 161 us
  matrix products  41.1 us (25%)
  local copies, waits for them, and re-layouts  40.3 us (25%)
  blocking collectives  39.9 us (25%)
  other arithmetic  18.4 us (11%)
  starting transfers between devices  12.1 us (7%)
  waiting for transfers between devices  9.11 us (6%)
    all_to_all x1, blocking collectives, copy_for_each(): return lax.all_to_all(copies, axis, split_axis=0, concat_axis=0, tiled=True)  25.9 us
    transpose x2, local copies, waits for them, and re-layouts, pair_einsum(): jnp.einsum('icf,jcf->ijf', left_part.astype(jnp.float32), right_part.asty...  22.9 us
    dot_general x1, matrix products, spectra_of(): spectrum = jnp.dot(flattened, basis, preferred_element_type=jnp.float32)  22.6 us
    all_to_all x1, blocking collectives, body(): parts = lax.all_to_all(parts, 'col', split_axis=0, concat_axis=0)  14 us
    dot_general x1, other arithmetic, similarity(): jnp.dot(cross_spec.reshape(left_rows * right_rows, 2 * half_len), inverse...  13.3 us
    all_to_all x1, starting transfers between devices, copy_for_each(): return lax.all_to_all(copies, axis, split_axis=0, concat_axis=0, tiled=True)  12.1 us
    dot_general x1, matrix products, similarity(): jnp.dot(cross_spec.reshape(left_rows * right_rows, 2 * half_len), inverse...  9.53 us
    all_to_all x1, waiting for transfers between devices, copy_for_each(): return lax.all_to_all(copies, axis, split_axis=0, concat_axis=0, tiled=True)  9.11 us
  transfers between devices with their start and end apart: 1, of which 1 were waited for; matrix products, arithmetic and copies ran while one was open for 11% of the time, Pallas kernels for 0%

profile of v1, /device:TPU:1, one launch (start us, length us, event | category | flops | bytes accessed | tf_op | source)
XLA Modules:
  0.0 161.1 jit_solution(16871548208129322738)
XLA Ops:
  0.0 0.9 multiply_reduce_fusion
  0.9 0.9 multiply_convert_fusion
  1.8 22.6 %fusion.20 = bf16[9,1280]{1,0:T(8,128)(2,1)S(1)} fusion(bf16[9,1024]{1,0:T(8,128)(2,1)S(1)} %reshape.450, bf16[1024]{0:T(1024)(128)(2,1)S(1)} %fusion.37, s32[1280]{0:T(1024)S(1)} %add_select_fusion.2, pred[1280]{0:T(1024)(128)(4,1)S(1)} %get-tuple-element.43, pred[1280]{0:T(1024)(128)(4,1)S(1)} %get-tuple-element.44), kind=kOutput, calls=%fused_computation.26 | convolution fusion | flops 39333120 | bytes 51200 | tf_op jit(solution)/shard_map/dot_general | solution.py:69
  24.5 0.1 broadcast_in_dim.105
  24.6 25.9 %all_to_all.15 = bf16[16,3,3,1280]{3,1,2,0:T(4,128)(2,1)S(1)} all-to-all(bf16[16,3,3,1280]{3,1,2,0:T(4,128)(2,1)S(1)} %broadcast_in_dim.105), channel_id=1, replica_groups=mesh['row'=16,'col'=32] {'row'}, dimensions={0} | all-to-all | bytes 737280 | tf_op jit(solution)/shard_map/all_to_all | solution.py:12
  50.5 1.2 broadcast_in_dim.108
  51.8 12.1 %all-to-all-start.1 = ((bf16[32,3,3,1280]{3,1,2,0:T(4,128)(2,1)}), bf16[32,3,3,1280]{3,1,2,0:T(4,128)(2,1)S(1)}, u32[]{:S(2)}, u32[]{:S(2)}) async-start(bf16[32,3,3,1280]{3,1,2,0:T(4,128)(2,1)} %broadcast_in_dim.108), calls=%async_computation.1 | async-start | bytes 1966080 | tf_op jit(solution)/shard_map/all_to_all | solution.py:12
  63.9 13.3 %select_convert_fusion.11 = bf16[1280,512]{1,0:T(8,128)(2,1)} fusion(f32[1280]{0:T(1024)S(1)} %get-tuple-element.46, bf16[512]{0:T(512)(128)(2,1)S(1)} %select_multiply_fusion.1, s32[512]{0:T(512)S(1)} %iota_add_fusion, s32[1280]{0:T(1024)S(1)} %add_select_fusion.2, f32[1280]{0:T(1024)S(1)} %get-tuple-element.45, ...), kind=kLoop, calls=%fused_computation.17.clone.clone.2 | loop fusion | flops 8519680 | bytes 1331712 | tf_op jit(solution)/shard_map/dot_general | solution.py:98
  77.2 0.2 copy.15
  77.4 0.3 reshape.452
  77.8 1.3 copy.22
  79.2 1.8 %copy.20 = bf16[48,6,640]{0,1,2:T(8,128)(2,1)} copy(bf16[48,6,640]{2,0,1:T(8,128)(2,1)S(1)} %pad_maximum_fusion.4) | data formatting | bytes 737280 | tf_op jit(solution)/shard_map/concatenate | solution.py:89
  81.0 9.1 %all-to-all-done.1 = bf16[32,3,3,1280]{3,1,2,0:T(4,128)(2,1)S(1)} async-done(((bf16[32,3,3,1280]{3,1,2,0:T(4,128)(2,1)}), bf16[32,3,3,1280]{3,1,2,0:T(4,128)(2,1)S(1)}, u32[]{:S(2)}, u32[]{:S(2)}) %all-to-all-start.1) | async-done | bytes 737312 | tf_op jit(solution)/shard_map/all_to_all | solution.py:12
  90.1 1.3 copy.17
  91.4 2.3 %reshape.453 = bf16[96,3,1280]{2,0,1:T(8,128)(2,1)S(1)} reshape(bf16[32,3,3,1280]{3,1,0,2:T(4,128)(2,1)} %copy.17) | data formatting | bytes 1474560 | tf_op jit(solution)/shard_map/reshape | solution.py:18
  93.7 0.8 fusion.50
  94.6 0.8 copy.26
  95.4 2.4 %broadcast_select_fusion = bf16[96,3,640]{0,1,2:T(4,128)(2,1)S(1)} fusion(bf16[96,3,640]{0,1,2:T(4,128)(2,1)S(1)} %copy.26, pred[640]{0:T(1024)(128)(4,1)S(1)} %iota_compare_fusion.2), kind=kLoop, calls=%fused_computation.41 | loop fusion | flops 184320 | bytes 737920 | tf_op jit(solution)/shard_map/jit(_where)/select_n | solution.py:85
  97.8 1.7 %copy.27 = bf16[96,3,640]{0,1,2:T(4,128)(2,1)S(1)} copy(bf16[96,3,640]{2,0,1:T(8,128)(2,1)} %get-tuple-element.6) | data formatting | bytes 737280
  99.4 4.5 %convert_bitcast_fusion = bf16[96,48,640]{0,1,2:T(8,128)(2,1)} fusion(bf16[48,6,640]{0,1,2:T(8,128)(2,1)S(1)} %copy.22, bf16[96,3,640]{0,1,2:T(4,128)(2,1)S(1)} %copy.27, bf16[96,3,640]{0,1,2:T(4,128)(2,1)S(1)} %broadcast_select_fusion), kind=kOutput, calls=%fused_computation.4 | convolution fusion | flops 39813120 | bytes 7004160 | tf_op jit(solution)/shard_map/icf,jcf->ijf/dot_general | solution.py:74
  103.9 11.4 %copy.23 = bf16[96,48,640]{2,1,0:T(8,128)(2,1)} copy(bf16[96,48,640]{0,1,2:T(8,128)(2,1)} %convert_bitcast_fusion) | data formatting | bytes 11796480 | tf_op jit(solution)/shard_map/icf,jcf->ijf/transpose | solution.py:74
  115.4 4.5 %convert_bitcast_fusion.1 = bf16[96,48,640]{0,1,2:T(8,128)(2,1)} fusion(bf16[48,6,640]{0,1,2:T(8,128)(2,1)S(1)} %copy-done, bf16[96,3,640]{0,1,2:T(4,128)(2,1)S(1)} %copy.27, bf16[96,3,640]{0,1,2:T(4,128)(2,1)S(1)} %copy.26), kind=kOutput, calls=%fused_computation.5 | convolution fusion | flops 39813120 | bytes 7004160 | tf_op jit(solution)/shard_map/icf,jcf->ijf/dot_general | solution.py:74
  119.8 11.5 %copy.21 = bf16[96,48,640]{2,1,0:T(8,128)(2,1)} copy(bf16[96,48,640]{0,1,2:T(8,128)(2,1)} %convert_bitcast_fusion.1) | data formatting | bytes 11796480 | tf_op jit(solution)/shard_map/icf,jcf->ijf/transpose | solution.py:74
  131.3 9.5 %fusion.17 = f32[4608]{0:T(1024)S(1)} fusion(bf16[4608,640]{1,0:T(8,128)(2,1)} %bitcast.21, bf16[4608,640]{1,0:T(8,128)(2,1)} %bitcast.22, bf16[1280,512]{1,0:T(8,128)(2,1)S(1)} %copy-done.1), kind=kOutput, calls=%fused_computation.25 | convolution fusion | flops 6065745408 | bytes 13125632 | tf_op jit(solution)/shard_map/dot_general | solution.py:98
  140.9 0.1 fusion.52
  141.0 0.1 fusion.51
  141.1 0.1 stack.99
  141.1 0.1 stack.100
  141.2 0.1 stack.101
  141.3 0.1 stack.102
  141.4 0.1 stack.103
  141.5 0.1 stack.104
  141.6 0.1 stack.105
  141.7 0.1 stack.107
  141.9 0.1 stack.109
  142.3 0.1 stack.114
  142.7 0.1 stack.119
  142.9 0.1 stack.121
  143.3 0.1 stack.126
  143.5 0.1 stack.128
  144.1 0.1 reshape.456
  144.2 14.0 %all_to_all.16 = f32[32,1,144]{2,1,0:T(1,128)S(1)} all-to-all(f32[32,1,144]{2,1,0:T(1,128)S(1)} %reshape.456), channel_id=1, replica_groups=mesh['row'=16,'col'=32] {'col'}, dimensions={0} | all-to-all | bytes 36864 | tf_op jit(solution)/shard_map/all_to_all | solution.py:120
  158.2 0.5 broadcast.247
  158.7 0.7 reduce
  159.4 0.1 reshape.457
  159.5 0.1 copy.24
  159.7 0.4 copy.25
  160.0 1.1 reshape.455
  (69 shorter events, 2.1 us)
Async XLA Ops:
  51.8 38.4 %all-to-all-start.1 = ((bf16[32,3,3,1280]{3,1,2,0:T(4,128)(2,1)}), bf16[32,3,3,1280]{3,1,2,0:T(4,128)(2,1)S(1)}, u32[]{:S(2)}, u32[]{:S(2)}) async-start(bf16[32,3,3,1280]{3,1,2,0:T(4,128)(2,1)} %broadcast_in_dim.108), calls=%async_computation.1 | async-start | bytes 1966080 | tf_op jit(solution)/shard_map/all_to_all | solution.py:12
  103.9 11.4 %copy-start = (bf16[48,6,640]{0,1,2:T(8,128)(2,1)S(1)}, bf16[48,6,640]{0,1,2:T(8,128)(2,1)}, u32[]{:S(2)}) copy-start(bf16[48,6,640]{0,1,2:T(8,128)(2,1)} %copy.20) | copy-start | bytes 1105924
  119.8 11.5 %copy-start.1 = (bf16[1280,512]{1,0:T(8,128)(2,1)S(1)}, bf16[1280,512]{1,0:T(8,128)(2,1)}, u32[]{:S(2)}) copy-start(bf16[1280,512]{1,0:T(8,128)(2,1)} %select_convert_fusion.11) | copy-start | bytes 3932164
